TPU v7x, 32 devices: a whole 2x2x4 slice. The times are simulated.
32 devices in a mesh: gx: 4 (over x, core), gy: 2 (over y), gz: 4 (over z).
Axes of the slice: x: 2, y: 2, z: 4, core: 2. Of those that a mesh axis runs over, the one named last changes fastest.
Arguments:
- velocity_rhs: float32 [3, 32, 32, 512], P(None, 'gz', 'gy', 'gx'), may hold values from -48 to 48
- pressure_rhs: float32 [16, 16, 256], P('gz', 'gy', 'gx'), may hold values from -6 to 6
- viscosity: float32 [32, 32, 512], P('gz', 'gy', 'gx'), may hold values from 0.6 to 1.4
- velocity_mass: float32 [32, 32, 512], P('gz', 'gy', 'gx'), may hold values from 0.5 to 4
- pressure_scale: float32 [16, 16, 256], P('gz', 'gy', 'gx'), may hold values from 0.6 to 1.5
- velocity_bounds: float32 [2], replicated, may hold values from 4 to 72, as said below
- pressure_bounds: float32 [2], replicated, may hold values from 0.08 to 2.8, as said below
Outputs:
- velocity: float32 [3, 32, 32, 512], P(None, 'gz', 'gy', 'gx')
- pressure: float32 [16, 16, 256], P('gz', 'gy', 'gx')
Inputs may be any that keep to these rules, and one draw needn't show every extreme that they name: velocity_bounds[0] is the lower bound and velocity_bounds[1] the upper one; the upper one exceeds the largest eigenvalue of A. pressure_bounds[0] is the lower bound and pressure_bounds[1] the upper one; the upper one exceeds the largest eigenvalue of M.
All inputs are finite; a program needn't handle non-finite values.
Results may differ from a plain program's by a relative error of at most 0.00002.
Values sent between devices are 32-bit elements; how exact they have to be, the bound alone decides.
A program may use at most 64 MiB of HBM per device.

v0:
```python
import jax
import jax.numpy as jnp
from jax import lax
from jax.sharding import PartitionSpec as P

SWEEPS = 2
PITERS = 2


def with_halo(value, sides, width):
    for axis, dim in sides:
        size, length = (lax.axis_size(axis), value.shape[dim])
        up = [(i, (i + 1) % size) for i in range(size - 1)]
        down = [(j, i) for i, j in up]
        last = lax.slice_in_dim(value, length - width, length, axis=dim)
        leading = lax.slice_in_dim(value, 0, width, axis=dim)
        before = lax.ppermute(last, axis, up)
        after = lax.ppermute(leading, axis, down)
        value = jnp.concatenate([before, value, after], axis=dim)
    return value


def pad_cells(field, width):
    return jnp.pad(field, [(0, 0)] * (field.ndim - 3) + [(width, width)] * 3)


def smooth_three(padded, outer_weight, centre):
    result = padded
    base = padded.ndim - 3
    for offset in range(3):
        dimension = base + offset
        length = result.shape[dimension] - 2
        result = (
            outer_weight * lax.slice_in_dim(result, 0, length, axis=dimension)
            + centre * lax.slice_in_dim(result, 1, length + 1, axis=dimension)
            + outer_weight * lax.slice_in_dim(result, 2, length + 2, axis=dimension)
        )
    return result


def chebyshev(source, operator, bounds, count):
    low_end = bounds[0]
    high_end = bounds[1]
    centre_value = (high_end + low_end) / 2.0
    spread = (high_end - low_end) / 2.0
    sigma_ratio = centre_value / spread
    factor = 1.0 / sigma_ratio
    direction = source / centre_value
    iterate = direction
    residual = source
    for repeat in range(count):
        residual = residual - operator(direction)
        factor_next = 1.0 / (2.0 * sigma_ratio - factor)
        direction = factor_next * factor * direction + 2.0 * factor_next / spread * residual
        iterate = iterate + direction
        factor = factor_next
    return iterate


def restrict_one(field, dimension):
    count = (field.shape[dimension] - 2) // 2
    return (
        0.25 * lax.slice_in_dim(field, 0, 2 * count, stride=2, axis=dimension)
        + 0.5 * lax.slice_in_dim(field, 1, 2 * count + 1, stride=2, axis=dimension)
        + 0.25 * lax.slice_in_dim(field, 2, 2 * count + 2, stride=2, axis=dimension)
    )


def divergence_restricted(padded):
    along_x = 0.5 * (padded[0, 1:-1, 1:-1, 2:] - padded[0, 1:-1, 1:-1, :-2])
    along_y = 0.5 * (padded[1, 1:-1, 2:, 1:-1] - padded[1, 1:-1, :-2, 1:-1])
    along_z = 0.5 * (padded[2, 2:, 1:-1, 1:-1] - padded[2, :-2, 1:-1, 1:-1])
    diverge = along_x + along_y + along_z
    for dimension in range(3):
        diverge = restrict_one(diverge, dimension)
    return diverge


def crop_cells(field, width):
    return field[..., width:-width, width:-width, width:-width]


def per_device(
    velocity_rhs,
    pressure_rhs,
    viscosity,
    velocity_mass,
    pressure_scale,
    velocity_bounds,
    pressure_bounds,
):
    stacked = jnp.concatenate([velocity_rhs, viscosity[None], velocity_mass[None]], axis=0)
    extended = with_halo(stacked, (("gx", 3), ("gy", 2), ("gz", 1)), SWEEPS + 2)
    source_wide = extended[:3]
    scale_wide = extended[3]
    mass_wide = extended[4]

    def apply_wide(direction):
        weighted = scale_wide * direction
        laplace = 16.0 * weighted - 2.0 * smooth_three(pad_cells(weighted, 1), 0.5, 1.0)
        return scale_wide * laplace + mass_wide * direction

    velocity_wide = chebyshev(source_wide, apply_wide, velocity_bounds, SWEEPS)
    velocity_padded = crop_cells(velocity_wide, SWEEPS)
    velocity = crop_cells(velocity_padded, 2)
    coupled = pressure_rhs - divergence_restricted(velocity_padded)

    def apply_pressure(direction):
        weighted = pressure_scale * direction
        padded = with_halo(weighted, (("gx", 2), ("gy", 1), ("gz", 0)), 1)
        return pressure_scale * smooth_three(padded, 1.0 / 6.0, 2.0 / 3.0)

    pressure = chebyshev(coupled, apply_pressure, pressure_bounds, PITERS)
    return (velocity, pressure)


def solution(mesh):
    in_specs = (
        P(None, "gz", "gy", "gx"),
        P("gz", "gy", "gx"),
        P("gz", "gy", "gx"),
        P("gz", "gy", "gx"),
        P("gz", "gy", "gx"),
        P(),
        P(),
    )
    out_specs = (P(None, "gz", "gy", "gx"), P("gz", "gy", "gx"))
    return jax.shard_map(
        per_device, mesh=mesh, in_specs=in_specs, out_specs=out_specs, check_vma=False
    )
```

profile of v0, /device:TPU:0, one launch (start us, length us, event | category | flops | bytes accessed | tf_op | source)
XLA Modules:
  0.0 94.2 jit_solution(2576197759723817899)
XLA Ops:
  1.9 2.4 %collective-permute-start = (f32[5,8,16,4]{3,2,1,0:T(8,128)S(1)}, f32[5,8,16,4]{3,2,1,0:T(8,128)S(1)}, u32[]{:S(2)}, u32[]{:S(2)}) collective-permute-start(f32[5,8,16,4]{3,2,1,0:T(8,128)S(1)} %get-tuple-element.10), channel_id=1, source_target_pairs={{0,8},{8,16},{16,24},{1,9},{9,17},{17,25},{2,10},{10,18},{18,26},{... | collective-permute-start | bytes 30728 | tf_op jit(solution)/shard_map/ppermute | solution.py:17
  4.3 1.3 %collective-permute-start.1 = (f32[5,8,16,4]{3,2,1,0:T(8,128)S(1)}, f32[5,8,16,4]{3,2,1,0:T(8,128)S(1)}, u32[]{:S(2)}, u32[]{:S(2)}) collective-permute-start(f32[5,8,16,4]{3,2,1,0:T(8,128)S(1)} %get-tuple-element.11), channel_id=1, source_target_pairs={{8,0},{16,8},{24,16},{9,1},{17,9},{25,17},{10,2},{18,10},{26,18},{... | collective-permute-start | bytes 30728 | tf_op jit(solution)/shard_map/ppermute | solution.py:18
  5.6 4.3 %collective-permute-done.1 = f32[5,8,16,4]{3,2,1,0:T(8,128)S(1)} collective-permute-done((f32[5,8,16,4]{3,2,1,0:T(8,128)S(1)}, f32[5,8,16,4]{3,2,1,0:T(8,128)S(1)}, u32[]{:S(2)}, u32[]{:S(2)}) %collective-permute-start.1) | collective-permute-done | bytes 10272 | tf_op jit(solution)/shard_map/ppermute | solution.py:18
  10.2 3.4 %collective-permute-start.2 = (f32[5,8,4,136]{3,2,1,0:T(4,128)S(1)}, f32[5,8,4,136]{3,2,1,0:T(4,128)S(1)}, u32[]{:S(2)}, u32[]{:S(2)}) collective-permute-start(f32[5,8,4,136]{3,2,1,0:T(4,128)S(1)} %get-tuple-element.8), channel_id=1, source_target_pairs={{0,4},{1,5},{2,6},{3,7},{8,12},{9,13},{10,14},{11,15},{16,20},{17,... | collective-permute-start | bytes 261128 | tf_op jit(solution)/shard_map/ppermute | solution.py:17
  13.7 1.3 %collective-permute-start.3 = (f32[5,8,4,136]{3,2,1,0:T(4,128)S(1)}, f32[5,8,4,136]{3,2,1,0:T(4,128)S(1)}, u32[]{:S(2)}, u32[]{:S(2)}) collective-permute-start(f32[5,8,4,136]{3,2,1,0:T(4,128)S(1)} %get-tuple-element.9), channel_id=1, source_target_pairs={{4,0},{5,1},{6,2},{7,3},{12,8},{13,9},{14,10},{15,11},{20,16},{21,... | collective-permute-start | bytes 261128 | tf_op jit(solution)/shard_map/ppermute | solution.py:18
  15.0 1.5 %collective-permute-done.2 = f32[5,8,4,136]{3,2,1,0:T(4,128)S(1)} collective-permute-done((f32[5,8,4,136]{3,2,1,0:T(4,128)S(1)}, f32[5,8,4,136]{3,2,1,0:T(4,128)S(1)}, u32[]{:S(2)}, u32[]{:S(2)}) %collective-permute-start.2) | collective-permute-done | bytes 87072 | tf_op jit(solution)/shard_map/ppermute | solution.py:17
  16.5 4.4 %collective-permute-done.3 = f32[5,8,4,136]{3,2,1,0:T(4,128)S(1)} collective-permute-done((f32[5,8,4,136]{3,2,1,0:T(4,128)S(1)}, f32[5,8,4,136]{3,2,1,0:T(4,128)S(1)}, u32[]{:S(2)}, u32[]{:S(2)}) %collective-permute-start.3) | collective-permute-done | bytes 87072 | tf_op jit(solution)/shard_map/ppermute | solution.py:18
  21.5 3.5 %collective-permute-start.4 = (f32[5,4,24,136]{3,2,1,0:T(8,128)S(1)}, f32[5,4,24,136]{3,2,1,0:T(8,128)S(1)}, u32[]{:S(2)}, u32[]{:S(2)}) collective-permute-start(f32[5,4,24,136]{3,2,1,0:T(8,128)S(1)} %get-tuple-element.6), channel_id=1, source_target_pairs={{0,1},{1,2},{2,3},{4,5},{5,6},{6,7},{8,9},{9,10},{10,11},{12,13},{... | collective-permute-start | bytes 783368 | tf_op jit(solution)/shard_map/ppermute | solution.py:17
  25.0 1.3 %collective-permute-start.5 = (f32[5,4,24,136]{3,2,1,0:T(8,128)S(1)}, f32[5,4,24,136]{3,2,1,0:T(8,128)S(1)}, u32[]{:S(2)}, u32[]{:S(2)}) collective-permute-start(f32[5,4,24,136]{3,2,1,0:T(8,128)S(1)} %get-tuple-element.7), channel_id=1, source_target_pairs={{1,0},{2,1},{3,2},{5,4},{6,5},{7,6},{9,8},{10,9},{11,10},{13,12},{... | collective-permute-start | bytes 783368 | tf_op jit(solution)/shard_map/ppermute | solution.py:18
  31.7 1.9 %collective-permute-done.4 = f32[5,4,24,136]{3,2,1,0:T(8,128)S(1)} collective-permute-done((f32[5,4,24,136]{3,2,1,0:T(8,128)S(1)}, f32[5,4,24,136]{3,2,1,0:T(8,128)S(1)}, u32[]{:S(2)}, u32[]{:S(2)}) %collective-permute-start.4) | collective-permute-done | bytes 261152 | tf_op jit(solution)/shard_map/ppermute | solution.py:17
  33.6 4.7 %collective-permute-done.5 = f32[5,4,24,136]{3,2,1,0:T(8,128)S(1)} collective-permute-done((f32[5,4,24,136]{3,2,1,0:T(8,128)S(1)}, f32[5,4,24,136]{3,2,1,0:T(8,128)S(1)}, u32[]{:S(2)}, u32[]{:S(2)}) %collective-permute-start.5) | collective-permute-done | bytes 261152 | tf_op jit(solution)/shard_map/ppermute | solution.py:18
  39.0 1.2 %fusion.2 = f32[3,16,26,138]{3,2,1,0:T(8,128)S(1)} fusion(f32[3,16,24,136]{3,2,1,0:T(8,128)S(1)} %broadcast_multiply_fusion), kind=kLoop, calls=%fused_computation.9 | loop fusion | flops 688896 | bytes 1315584 | tf_op jit(solution)/shard_map/add | solution.py:34
  41.4 1.2 %fusion.6 = f32[3,16,26,138]{3,2,1,0:T(8,128)S(1)} fusion(f32[3,16,24,136]{3,2,1,0:T(8,128)S(1)} %fusion.25), kind=kLoop, calls=%fused_computation.13 | loop fusion | flops 688896 | bytes 1315584 | tf_op jit(solution)/shard_map/add | solution.py:34
  42.9 1.7 %fusion.16 = f32[3,16,24,136]{3,2,1,0:T(8,128)S(1)} fusion(f32[3,16,24,138]{3,2,1,0:T(8,128)S(1)} %fusion.17, f32[]{:T(128)S(6)} %div.79, f32[]{:T(128)S(6)} %mul.301, f32[16,24,136]{2,1,0:T(8,128)S(1)} %get-tuple-element.4, f32[16,24,136]{2,1,0:T(8,128)S(1)} %get-tuple-element.5, f32[]{:T(128)S(6)} %div.77, f32[]{:T(128)S(6)} %mul.280, ...), kind=kLoop, calls=%fused_computation.24 | loop fusion | flops 5170176 | bytes 5431316 | tf_op jit(solution)/shard_map/add | solution.py:55
  46.4 4.4 %collective-permute-start.6 = (f32[4,8,1]{2,1,0:T(8,128)S(1)}, f32[4,8,1]{2,1,0:T(8,128)S(1)}, u32[]{:S(2)}, u32[]{:S(2)}) collective-permute-start(f32[4,8,1]{2,1,0:T(8,128)S(1)} %get-tuple-element.22), channel_id=1, source_target_pairs={{0,8},{8,16},{16,24},{1,9},{9,17},{17,25},{2,10},{10,18},{18,26},{... | collective-permute-start | bytes 392 | tf_op jit(solution)/shard_map/ppermute | solution.py:17
  50.8 1.3 %collective-permute-start.7 = (f32[4,8,1]{2,1,0:T(8,128)S(1)}, f32[4,8,1]{2,1,0:T(8,128)S(1)}, u32[]{:S(2)}, u32[]{:S(2)}) collective-permute-start(f32[4,8,1]{2,1,0:T(8,128)S(1)} %get-tuple-element.23), channel_id=1, source_target_pairs={{8,0},{16,8},{24,16},{9,1},{17,9},{25,17},{10,2},{18,10},{26,18},{... | collective-permute-start | bytes 392 | tf_op jit(solution)/shard_map/ppermute | solution.py:18
  52.2 1.8 %collective-permute-done.7 = f32[4,8,1]{2,1,0:T(8,128)S(1)} collective-permute-done((f32[4,8,1]{2,1,0:T(8,128)S(1)}, f32[4,8,1]{2,1,0:T(8,128)S(1)}, u32[]{:S(2)}, u32[]{:S(2)}) %collective-permute-start.7) | collective-permute-done | bytes 160 | tf_op jit(solution)/shard_map/ppermute | solution.py:18
  54.0 1.4 %collective-permute-start.8 = (f32[4,1,66]{2,1,0:T(1,128)S(1)}, f32[4,1,66]{2,1,0:T(1,128)S(1)}, u32[]{:S(2)}, u32[]{:S(2)}) collective-permute-start(f32[4,1,66]{2,1,0:T(1,128)S(1)} %get-tuple-element.14), channel_id=1, source_target_pairs={{0,4},{1,5},{2,6},{3,7},{8,12},{9,13},{10,14},{11,15},{16,20},{17,... | collective-permute-start | bytes 3176 | tf_op jit(solution)/shard_map/ppermute | solution.py:17
  55.5 1.3 %collective-permute-start.9 = (f32[4,1,66]{2,1,0:T(1,128)S(1)}, f32[4,1,66]{2,1,0:T(1,128)S(1)}, u32[]{:S(2)}, u32[]{:S(2)}) collective-permute-start(f32[4,1,66]{2,1,0:T(1,128)S(1)} %get-tuple-element.15), channel_id=1, source_target_pairs={{4,0},{5,1},{6,2},{7,3},{12,8},{13,9},{14,10},{15,11},{20,16},{21,... | collective-permute-start | bytes 3176 | tf_op jit(solution)/shard_map/ppermute | solution.py:18
  56.8 4.2 %collective-permute-done.9 = f32[4,1,66]{2,1,0:T(1,128)S(1)} collective-permute-done((f32[4,1,66]{2,1,0:T(1,128)S(1)}, f32[4,1,66]{2,1,0:T(1,128)S(1)}, u32[]{:S(2)}, u32[]{:S(2)}) %collective-permute-start.9) | collective-permute-done | bytes 1088 | tf_op jit(solution)/shard_map/ppermute | solution.py:18
  61.0 3.5 %collective-permute-start.10 = (f32[1,10,66]{2,1,0:T(8,128)S(1)}, f32[1,10,66]{2,1,0:T(8,128)S(1)}, u32[]{:S(2)}, u32[]{:S(2)}) collective-permute-start(f32[1,10,66]{2,1,0:T(8,128)S(1)} %get-tuple-element.18), channel_id=1, source_target_pairs={{0,1},{1,2},{2,3},{4,5},{5,6},{6,7},{8,9},{9,10},{10,11},{12,13},{... | collective-permute-start | bytes 7928 | tf_op jit(solution)/shard_map/ppermute | solution.py:17
  64.5 1.3 %collective-permute-start.11 = (f32[1,10,66]{2,1,0:T(8,128)S(1)}, f32[1,10,66]{2,1,0:T(8,128)S(1)}, u32[]{:S(2)}, u32[]{:S(2)}) collective-permute-start(f32[1,10,66]{2,1,0:T(8,128)S(1)} %get-tuple-element.19), channel_id=1, source_target_pairs={{1,0},{2,1},{3,2},{5,4},{6,5},{7,6},{9,8},{10,9},{11,10},{13,12},{... | collective-permute-start | bytes 7928 | tf_op jit(solution)/shard_map/ppermute | solution.py:18
  67.3 2.7 %collective-permute-done.11 = f32[1,10,66]{2,1,0:T(8,128)S(1)} collective-permute-done((f32[1,10,66]{2,1,0:T(8,128)S(1)}, f32[1,10,66]{2,1,0:T(8,128)S(1)}, u32[]{:S(2)}, u32[]{:S(2)}) %collective-permute-start.11) | collective-permute-done | bytes 2672 | tf_op jit(solution)/shard_map/ppermute | solution.py:18
  70.3 1.3 %collective-permute-start.12 = (f32[4,8,1]{2,1,0:T(8,128)S(1)}, f32[4,8,1]{2,1,0:T(8,128)S(1)}, u32[]{:S(2)}, u32[]{:S(2)}) collective-permute-start(f32[4,8,1]{2,1,0:T(8,128)S(1)} %get-tuple-element.20), channel_id=1, source_target_pairs={{0,8},{8,16},{16,24},{1,9},{9,17},{17,25},{2,10},{10,18},{18,26},{... | collective-permute-start | bytes 392 | tf_op jit(solution)/shard_map/ppermute | solution.py:17
  71.6 1.3 %collective-permute-start.13 = (f32[4,8,1]{2,1,0:T(8,128)S(1)}, f32[4,8,1]{2,1,0:T(8,128)S(1)}, u32[]{:S(2)}, u32[]{:S(2)}) collective-permute-start(f32[4,8,1]{2,1,0:T(8,128)S(1)} %get-tuple-element.21), channel_id=1, source_target_pairs={{8,0},{16,8},{24,16},{9,1},{17,9},{25,17},{10,2},{18,10},{26,18},{... | collective-permute-start | bytes 392 | tf_op jit(solution)/shard_map/ppermute | solution.py:18
  73.0 4.0 %collective-permute-done.13 = f32[4,8,1]{2,1,0:T(8,128)S(1)} collective-permute-done((f32[4,8,1]{2,1,0:T(8,128)S(1)}, f32[4,8,1]{2,1,0:T(8,128)S(1)}, u32[]{:S(2)}, u32[]{:S(2)}) %collective-permute-start.13) | collective-permute-done | bytes 160 | tf_op jit(solution)/shard_map/ppermute | solution.py:18
  77.1 1.7 %collective-permute-start.14 = (f32[4,1,66]{2,1,0:T(1,128)S(1)}, f32[4,1,66]{2,1,0:T(1,128)S(1)}, u32[]{:S(2)}, u32[]{:S(2)}) collective-permute-start(f32[4,1,66]{2,1,0:T(1,128)S(1)} %get-tuple-element.12), channel_id=1, source_target_pairs={{0,4},{1,5},{2,6},{3,7},{8,12},{9,13},{10,14},{11,15},{16,20},{17,... | collective-permute-start | bytes 3176 | tf_op jit(solution)/shard_map/ppermute | solution.py:17
  78.7 1.3 %collective-permute-start.15 = (f32[4,1,66]{2,1,0:T(1,128)S(1)}, f32[4,1,66]{2,1,0:T(1,128)S(1)}, u32[]{:S(2)}, u32[]{:S(2)}) collective-permute-start(f32[4,1,66]{2,1,0:T(1,128)S(1)} %get-tuple-element.13), channel_id=1, source_target_pairs={{4,0},{5,1},{6,2},{7,3},{12,8},{13,9},{14,10},{15,11},{20,16},{21,... | collective-permute-start | bytes 3176 | tf_op jit(solution)/shard_map/ppermute | solution.py:18
  80.0 4.2 %collective-permute-done.15 = f32[4,1,66]{2,1,0:T(1,128)S(1)} collective-permute-done((f32[4,1,66]{2,1,0:T(1,128)S(1)}, f32[4,1,66]{2,1,0:T(1,128)S(1)}, u32[]{:S(2)}, u32[]{:S(2)}) %collective-permute-start.15) | collective-permute-done | bytes 1088 | tf_op jit(solution)/shard_map/ppermute | solution.py:18
  84.3 3.5 %collective-permute-start.16 = (f32[1,10,66]{2,1,0:T(8,128)S(1)}, f32[1,10,66]{2,1,0:T(8,128)S(1)}, u32[]{:S(2)}, u32[]{:S(2)}) collective-permute-start(f32[1,10,66]{2,1,0:T(8,128)S(1)} %get-tuple-element.16), channel_id=1, source_target_pairs={{0,1},{1,2},{2,3},{4,5},{5,6},{6,7},{8,9},{9,10},{10,11},{12,13},{... | collective-permute-start | bytes 7928 | tf_op jit(solution)/shard_map/ppermute | solution.py:17
  87.8 1.3 %collective-permute-start.17 = (f32[1,10,66]{2,1,0:T(8,128)S(1)}, f32[1,10,66]{2,1,0:T(8,128)S(1)}, u32[]{:S(2)}, u32[]{:S(2)}) collective-permute-start(f32[1,10,66]{2,1,0:T(8,128)S(1)} %get-tuple-element.17), channel_id=1, source_target_pairs={{1,0},{2,1},{3,2},{5,4},{6,5},{7,6},{9,8},{10,9},{11,10},{13,12},{... | collective-permute-start | bytes 7928 | tf_op jit(solution)/shard_map/ppermute | solution.py:18
  90.0 3.4 %collective-permute-done.17 = f32[1,10,66]{2,1,0:T(8,128)S(1)} collective-permute-done((f32[1,10,66]{2,1,0:T(8,128)S(1)}, f32[1,10,66]{2,1,0:T(8,128)S(1)}, u32[]{:S(2)}, u32[]{:S(2)}) %collective-permute-start.17) | collective-permute-done | bytes 2672 | tf_op jit(solution)/shard_map/ppermute | solution.py:18
  (59 shorter events, 9.4 us)
Async XLA Ops:
  0.6 9.3 %copy-start.2 = (f32[8,16,128]{2,1,0:T(8,128)S(1)}, f32[8,16,128]{2,1,0:T(8,128)}, u32[]{:S(2)}) copy-start(f32[8,16,128]{2,1,0:T(8,128)} %param.9) | copy-start | bytes 196612
  0.6 9.3 %copy-start.1 = (f32[8,16,128]{2,1,0:T(8,128)S(1)}, f32[8,16,128]{2,1,0:T(8,128)}, u32[]{:S(2)}) copy-start(f32[8,16,128]{2,1,0:T(8,128)} %param.10) | copy-start | bytes 196612
  0.7 9.3 %copy-start = (f32[3,8,16,128]{3,2,1,0:T(8,128)S(1)}, f32[3,8,16,128]{3,2,1,0:T(8,128)}, u32[]{:S(2)}) copy-start(f32[3,8,16,128]{3,2,1,0:T(8,128)} %param.7) | copy-start | bytes 589828
  1.9 3.7 %collective-permute-start = (f32[5,8,16,4]{3,2,1,0:T(8,128)S(1)}, f32[5,8,16,4]{3,2,1,0:T(8,128)S(1)}, u32[]{:S(2)}, u32[]{:S(2)}) collective-permute-start(f32[5,8,16,4]{3,2,1,0:T(8,128)S(1)} %get-tuple-element.10), channel_id=1, source_target_pairs={{0,8},{8,16},{16,24},{1,9},{9,17},{17,25},{2,10},{10,18},{18,26},{... | collective-permute-start | bytes 30728 | tf_op jit(solution)/shard_map/ppermute | solution.py:17
  4.3 5.6 %collective-permute-start.1 = (f32[5,8,16,4]{3,2,1,0:T(8,128)S(1)}, f32[5,8,16,4]{3,2,1,0:T(8,128)S(1)}, u32[]{:S(2)}, u32[]{:S(2)}) collective-permute-start(f32[5,8,16,4]{3,2,1,0:T(8,128)S(1)} %get-tuple-element.11), channel_id=1, source_target_pairs={{8,0},{16,8},{24,16},{9,1},{17,9},{25,17},{10,2},{18,10},{26,18},{... | collective-permute-start | bytes 30728 | tf_op jit(solution)/shard_map/ppermute | solution.py:18
  10.2 6.3 %collective-permute-start.2 = (f32[5,8,4,136]{3,2,1,0:T(4,128)S(1)}, f32[5,8,4,136]{3,2,1,0:T(4,128)S(1)}, u32[]{:S(2)}, u32[]{:S(2)}) collective-permute-start(f32[5,8,4,136]{3,2,1,0:T(4,128)S(1)} %get-tuple-element.8), channel_id=1, source_target_pairs={{0,4},{1,5},{2,6},{3,7},{8,12},{9,13},{10,14},{11,15},{16,20},{17,... | collective-permute-start | bytes 261128 | tf_op jit(solution)/shard_map/ppermute | solution.py:17
  13.7 7.2 %collective-permute-start.3 = (f32[5,8,4,136]{3,2,1,0:T(4,128)S(1)}, f32[5,8,4,136]{3,2,1,0:T(4,128)S(1)}, u32[]{:S(2)}, u32[]{:S(2)}) collective-permute-start(f32[5,8,4,136]{3,2,1,0:T(4,128)S(1)} %get-tuple-element.9), channel_id=1, source_target_pairs={{4,0},{5,1},{6,2},{7,3},{12,8},{13,9},{14,10},{15,11},{20,16},{21,... | collective-permute-start | bytes 261128 | tf_op jit(solution)/shard_map/ppermute | solution.py:18
  21.4 4.9 %copy-start.5 = (f32[2]{0:T(128)S(1)}, f32[2]{0:T(128)}, u32[]{:S(2)}) copy-start(f32[2]{0:T(128)} %param.12) | copy-start | bytes 28
  21.4 8.4 %copy-start.6 = (f32[2]{0:T(128)S(1)}, f32[2]{0:T(128)}, u32[]{:S(2)}) copy-start(f32[2]{0:T(128)} %param.13) | copy-start | bytes 28
  21.5 12.1 %collective-permute-start.4 = (f32[5,4,24,136]{3,2,1,0:T(8,128)S(1)}, f32[5,4,24,136]{3,2,1,0:T(8,128)S(1)}, u32[]{:S(2)}, u32[]{:S(2)}) collective-permute-start(f32[5,4,24,136]{3,2,1,0:T(8,128)S(1)} %get-tuple-element.6), channel_id=1, source_target_pairs={{0,1},{1,2},{2,3},{4,5},{5,6},{6,7},{8,9},{9,10},{10,11},{12,13},{... | collective-permute-start | bytes 783368 | tf_op jit(solution)/shard_map/ppermute | solution.py:17
  25.0 13.3 %collective-permute-start.5 = (f32[5,4,24,136]{3,2,1,0:T(8,128)S(1)}, f32[5,4,24,136]{3,2,1,0:T(8,128)S(1)}, u32[]{:S(2)}, u32[]{:S(2)}) collective-permute-start(f32[5,4,24,136]{3,2,1,0:T(8,128)S(1)} %get-tuple-element.7), channel_id=1, source_target_pairs={{1,0},{2,1},{3,2},{5,4},{6,5},{7,6},{9,8},{10,9},{11,10},{13,12},{... | collective-permute-start | bytes 783368 | tf_op jit(solution)/shard_map/ppermute | solution.py:18
  44.7 1.6 %copy-start.3 = (f32[4,8,64]{2,1,0:T(8,128)S(1)}, f32[4,8,64]{2,1,0:T(8,128)}, u32[]{:S(2)}) copy-start(f32[4,8,64]{2,1,0:T(8,128)} %param.11) | copy-start | bytes 24580
  44.7 1.6 %copy-start.4 = (f32[4,8,64]{2,1,0:T(8,128)S(1)}, f32[4,8,64]{2,1,0:T(8,128)}, u32[]{:S(2)}) copy-start(f32[4,8,64]{2,1,0:T(8,128)} %param.8) | copy-start | bytes 24580
  46.4 5.7 %collective-permute-start.6 = (f32[4,8,1]{2,1,0:T(8,128)S(1)}, f32[4,8,1]{2,1,0:T(8,128)S(1)}, u32[]{:S(2)}, u32[]{:S(2)}) collective-permute-start(f32[4,8,1]{2,1,0:T(8,128)S(1)} %get-tuple-element.22), channel_id=1, source_target_pairs={{0,8},{8,16},{16,24},{1,9},{9,17},{17,25},{2,10},{10,18},{18,26},{... | collective-permute-start | bytes 392 | tf_op jit(solution)/shard_map/ppermute | solution.py:17
  50.8 3.1 %collective-permute-start.7 = (f32[4,8,1]{2,1,0:T(8,128)S(1)}, f32[4,8,1]{2,1,0:T(8,128)S(1)}, u32[]{:S(2)}, u32[]{:S(2)}) collective-permute-start(f32[4,8,1]{2,1,0:T(8,128)S(1)} %get-tuple-element.23), channel_id=1, source_target_pairs={{8,0},{16,8},{24,16},{9,1},{17,9},{25,17},{10,2},{18,10},{26,18},{... | collective-permute-start | bytes 392 | tf_op jit(solution)/shard_map/ppermute | solution.py:18
  54.0 2.8 %collective-permute-start.8 = (f32[4,1,66]{2,1,0:T(1,128)S(1)}, f32[4,1,66]{2,1,0:T(1,128)S(1)}, u32[]{:S(2)}, u32[]{:S(2)}) collective-permute-start(f32[4,1,66]{2,1,0:T(1,128)S(1)} %get-tuple-element.14), channel_id=1, source_target_pairs={{0,4},{1,5},{2,6},{3,7},{8,12},{9,13},{10,14},{11,15},{16,20},{17,... | collective-permute-start | bytes 3176 | tf_op jit(solution)/shard_map/ppermute | solution.py:17
  55.5 5.5 %collective-permute-start.9 = (f32[4,1,66]{2,1,0:T(1,128)S(1)}, f32[4,1,66]{2,1,0:T(1,128)S(1)}, u32[]{:S(2)}, u32[]{:S(2)}) collective-permute-start(f32[4,1,66]{2,1,0:T(1,128)S(1)} %get-tuple-element.15), channel_id=1, source_target_pairs={{4,0},{5,1},{6,2},{7,3},{12,8},{13,9},{14,10},{15,11},{20,16},{21,... | collective-permute-start | bytes 3176 | tf_op jit(solution)/shard_map/ppermute | solution.py:18
  61.0 6.3 %collective-permute-start.10 = (f32[1,10,66]{2,1,0:T(8,128)S(1)}, f32[1,10,66]{2,1,0:T(8,128)S(1)}, u32[]{:S(2)}, u32[]{:S(2)}) collective-permute-start(f32[1,10,66]{2,1,0:T(8,128)S(1)} %get-tuple-element.18), channel_id=1, source_target_pairs={{0,1},{1,2},{2,3},{4,5},{5,6},{6,7},{8,9},{9,10},{10,11},{12,13},{... | collective-permute-start | bytes 7928 | tf_op jit(solution)/shard_map/ppermute | solution.py:17
  64.5 5.5 %collective-permute-start.11 = (f32[1,10,66]{2,1,0:T(8,128)S(1)}, f32[1,10,66]{2,1,0:T(8,128)S(1)}, u32[]{:S(2)}, u32[]{:S(2)}) collective-permute-start(f32[1,10,66]{2,1,0:T(8,128)S(1)} %get-tuple-element.19), channel_id=1, source_target_pairs={{1,0},{2,1},{3,2},{5,4},{6,5},{7,6},{9,8},{10,9},{11,10},{13,12},{... | collective-permute-start | bytes 7928 | tf_op jit(solution)/shard_map/ppermute | solution.py:18
  70.3 2.6 %collective-permute-start.12 = (f32[4,8,1]{2,1,0:T(8,128)S(1)}, f32[4,8,1]{2,1,0:T(8,128)S(1)}, u32[]{:S(2)}, u32[]{:S(2)}) collective-permute-start(f32[4,8,1]{2,1,0:T(8,128)S(1)} %get-tuple-element.20), channel_id=1, source_target_pairs={{0,8},{8,16},{16,24},{1,9},{9,17},{17,25},{2,10},{10,18},{18,26},{... | collective-permute-start | bytes 392 | tf_op jit(solution)/shard_map/ppermute | solution.py:17
  71.6 5.3 %collective-permute-start.13 = (f32[4,8,1]{2,1,0:T(8,128)S(1)}, f32[4,8,1]{2,1,0:T(8,128)S(1)}, u32[]{:S(2)}, u32[]{:S(2)}) collective-permute-start(f32[4,8,1]{2,1,0:T(8,128)S(1)} %get-tuple-element.21), channel_id=1, source_target_pairs={{8,0},{16,8},{24,16},{9,1},{17,9},{25,17},{10,2},{18,10},{26,18},{... | collective-permute-start | bytes 392 | tf_op jit(solution)/shard_map/ppermute | solution.py:18
  77.1 3.0 %collective-permute-start.14 = (f32[4,1,66]{2,1,0:T(1,128)S(1)}, f32[4,1,66]{2,1,0:T(1,128)S(1)}, u32[]{:S(2)}, u32[]{:S(2)}) collective-permute-start(f32[4,1,66]{2,1,0:T(1,128)S(1)} %get-tuple-element.12), channel_id=1, source_target_pairs={{0,4},{1,5},{2,6},{3,7},{8,12},{9,13},{10,14},{11,15},{16,20},{17,... | collective-permute-start | bytes 3176 | tf_op jit(solution)/shard_map/ppermute | solution.py:17
  78.7 5.5 %collective-permute-start.15 = (f32[4,1,66]{2,1,0:T(1,128)S(1)}, f32[4,1,66]{2,1,0:T(1,128)S(1)}, u32[]{:S(2)}, u32[]{:S(2)}) collective-permute-start(f32[4,1,66]{2,1,0:T(1,128)S(1)} %get-tuple-element.13), channel_id=1, source_target_pairs={{4,0},{5,1},{6,2},{7,3},{12,8},{13,9},{14,10},{15,11},{20,16},{21,... | collective-permute-start | bytes 3176 | tf_op jit(solution)/shard_map/ppermute | solution.py:18
  84.3 5.7 %collective-permute-start.16 = (f32[1,10,66]{2,1,0:T(8,128)S(1)}, f32[1,10,66]{2,1,0:T(8,128)S(1)}, u32[]{:S(2)}, u32[]{:S(2)}) collective-permute-start(f32[1,10,66]{2,1,0:T(8,128)S(1)} %get-tuple-element.16), channel_id=1, source_target_pairs={{0,1},{1,2},{2,3},{4,5},{5,6},{6,7},{8,9},{9,10},{10,11},{12,13},{... | collective-permute-start | bytes 7928 | tf_op jit(solution)/shard_map/ppermute | solution.py:17
  87.8 5.5 %collective-permute-start.17 = (f32[1,10,66]{2,1,0:T(8,128)S(1)}, f32[1,10,66]{2,1,0:T(8,128)S(1)}, u32[]{:S(2)}, u32[]{:S(2)}) collective-permute-start(f32[1,10,66]{2,1,0:T(8,128)S(1)} %get-tuple-element.17), channel_id=1, source_target_pairs={{1,0},{2,1},{3,2},{5,4},{6,5},{7,6},{9,8},{10,9},{11,10},{13,12},{... | collective-permute-start | bytes 7928 | tf_op jit(solution)/shard_map/ppermute | solution.py:18
where the time goes:
time: 94.8 us; the launch traced here: 94.2 us
  waiting for transfers between devices  37 us (39%)
  starting transfers between devices  36.7 us (39%)
  other arithmetic  9.98 us (11%)
  between operations  6.88 us (7%)
  local copies, waits for them, and re-layouts  3.6 us (4%)
    ppermute x9, waiting for transfers between devices, with_halo(): after = lax.ppermute(leading, axis, down)  33.6 us
    ppermute x9, starting transfers between devices, with_halo(): before = lax.ppermute(last, axis, up)  25.1 us
    ppermute x9, starting transfers between devices, with_halo(): after = lax.ppermute(leading, axis, down)  11.6 us
    ppermute x9, waiting for transfers between devices, with_halo(): before = lax.ppermute(last, axis, up)  3.39 us
    add x8, other arithmetic, smooth_three(): outer_weight * lax.slice_in_dim(result, 0, length, axis=dimension)  3.33 us
    add x2, other arithmetic, chebyshev(): iterate = iterate + direction  2.44 us
  transfers between devices with their start and end apart: 18, of which 11 were waited for; matrix products, arithmetic and copies ran while one was open for 2% of the time, Pallas kernels for 0%

commit v1 on v0

v1 whole, which is shorter than its diff:
```python
import itertools

import jax
import jax.numpy as jnp
from jax import lax
from jax.experimental import pallas as pl
from jax.experimental.pallas import tpu as pltpu
from jax.sharding import PartitionSpec as P

SWEEPS = 2
PITERS = 2
BELOW = SWEEPS + 2
ABOVE = SWEEPS + 1
ROWS = 8
FIELDS = 5
GROUP = 8
MESH = pl.DeviceIdType.MESH
AXES = ("gx", "gy", "gz")
DIRECTIONS = [d for d in itertools.product((0, -1, 1), repeat=3) if d != (0, 0, 0)]
DIRECTIONS.sort(key=lambda d: -sum(abs(c) for c in d))


def chebyshev_scalars(bounds, count):
    low, high = bounds[0], bounds[1]
    theta = (high + low) * 0.5
    delta = (high - low) * 0.5
    sigma = theta / delta
    rho = 1.0 / sigma
    steps = []
    for _ in range(count):
        rho_next = 1.0 / (2.0 * sigma - rho)
        steps.append((rho_next * rho, 2.0 * rho_next / delta))
        rho = rho_next
    return 1.0 / theta, steps


def average(value, axis, outer, centre):
    size = value.shape[axis]
    return centre * value + outer * (pltpu.roll(value, 1, axis) + pltpu.roll(value, size - 1, axis))


def kernel(
    vrhs, prhs, visc, mass, pscale, vbounds, pbounds,
    vout, pout,
    main, left, right, packed,
    wide_b, wide_v, wide_m, smooth, smooth_next, resid, direct, total,
    gathered, prhs_in, pscale_in, scale_all, coupled_all, to_pressure, rows_at, vres, pres,
    local_sem, send_sem, recv_sem,
):
    nz, ny, nx = visc.shape
    pz, py, px = pscale.shape
    depth = BELOW + nz + ABOVE
    sizes = [lax.axis_size(a) for a in AXES]
    at = [lax.axis_index(a) for a in AXES]

    def exists(d):
        ok = None
        for coordinate, place, size in zip(d, at, sizes):
            if coordinate:
                here = place > 0 if coordinate < 0 else place < size - 1
                ok = here if ok is None else jnp.logical_and(ok, here)
        return ok

    def target(d):
        return {a: p + c for a, p, c in zip(AXES, at, d)}

    mid = pl.ds(BELOW, nz)
    loads = [
        pltpu.make_async_copy(vrhs, main.at[pl.ds(0, 3), mid, pl.ds(0, ny), :], local_sem.at[0]),
        pltpu.make_async_copy(visc, main.at[3, mid, pl.ds(0, ny), :], local_sem.at[1]),
        pltpu.make_async_copy(mass, main.at[4, mid, pl.ds(0, ny), :], local_sem.at[2]),
        pltpu.make_async_copy(pscale, pscale_in, local_sem.at[3]),
        pltpu.make_async_copy(prhs, prhs_in, local_sem.at[4]),
    ]
    for load in loads:
        load.start()

    for f in range(FIELDS):
        main[f, pl.ds(0, BELOW)] = jnp.zeros((BELOW, ny + 2 * ROWS, nx), jnp.float32)
        main[f, pl.ds(BELOW + nz, ABOVE)] = jnp.zeros((ABOVE, ny + 2 * ROWS, nx), jnp.float32)
        main[f, mid, pl.ds(ny, 2 * ROWS)] = jnp.zeros((nz, 2 * ROWS, nx), jnp.float32)
    left[...] = jnp.zeros_like(left)
    right[...] = jnp.zeros_like(right)
    scale_all[...] = jnp.zeros_like(scale_all)
    coupled_all[...] = jnp.zeros_like(coupled_all)

    barrier = pltpu.get_barrier_semaphore()
    count = None
    for place, size in zip(at, sizes):
        span = 1 + jnp.where(place > 0, 1, 0) + jnp.where(place < size - 1, 1, 0)
        count = span if count is None else count * span
    for d in DIRECTIONS:
        @pl.when(exists(d))
        def _(d=d):
            pl.semaphore_signal(barrier, inc=1, device_id=target(d), device_id_type=MESH)

    x_at = lax.broadcasted_iota(jnp.int32, (2 * nx, 2 * px), 0)
    x_at = jnp.where(x_at < nx + nx // 2, x_at, x_at - 2 * nx)
    column = lax.broadcasted_iota(jnp.int32, (2 * nx, 2 * px), 1)
    offset = x_at - 2 * jnp.where(column < px, column, column - px)
    apart = jnp.where(offset < 0, -offset, offset)
    to_pressure[0] = jnp.where(apart == 0, 0.5, jnp.where(apart == 1, 0.25, 0.0))
    slope = jnp.where(apart == 1, 0.25, jnp.where(apart == 2, 0.125, 0.0))
    to_pressure[1] = jnp.where(offset < 0, -slope, slope)

    for load in loads:
        load.wait()

    lane = lax.broadcasted_iota(jnp.int32, (ny, nx), 1)

    @pl.loop(0, nz)
    def _(k):
        edge = main[0, BELOW + k, pl.ds(0, ny), :]
        for f in range(1, FIELDS):
            moved = pltpu.roll(main[f, BELOW + k, pl.ds(0, ny), :], GROUP * f, 1)
            inside = jnp.logical_and(lane >= GROUP * f - BELOW, lane < GROUP * f + BELOW)
            edge = jnp.where(inside, moved, edge)
        packed[k] = edge

    scale_own = pscale_in[...]
    scale_all[1, pl.ds(PITERS, pz), pl.ds(0, py), :] = jnp.concatenate([scale_own, scale_own], axis=2)

    pl.semaphore_wait(barrier, count - 1)

    def velocity_copy(d):
        dx, dy, dz = d
        z_from, z_to, z_many = {
            0: (BELOW, BELOW, nz), 1: (nz, 0, BELOW), -1: (BELOW, BELOW + nz, ABOVE)}[dz]
        y_from, y_to, y_many = {
            0: (0, 0, ny), 1: (ny - ROWS, ny + ROWS, ROWS), -1: (0, ny, ROWS)}[dy]
        if dx == 0:
            source = main.at[:, pl.ds(z_from, z_many), pl.ds(y_from, y_many), :]
            place = main.at[:, pl.ds(z_to, z_many), pl.ds(y_to, y_many), :]
        else:
            source = packed.at[pl.ds(z_from - BELOW, z_many), pl.ds(y_from, y_many), :]
            place = (left if dx == 1 else right).at[pl.ds(z_to, z_many), pl.ds(y_to, y_many), :]
        at_sem = DIRECTIONS.index(d)
        return pltpu.make_async_remote_copy(
            src_ref=source, dst_ref=place, send_sem=send_sem.at[0, at_sem],
            recv_sem=recv_sem.at[0, at_sem], device_id=target(d), device_id_type=MESH)

    def pressure_copy(buffer, which, d):
        dx, dy, dz = d
        z_from, z_to, z_many = {
            0: (PITERS, PITERS, pz), 1: (pz, 0, PITERS), -1: (PITERS, PITERS + pz, PITERS)}[dz]
        y_to = {0: 0, 1: 2 * ROWS, -1: ROWS}[dy]
        at_sem = DIRECTIONS.index(d)
        return pltpu.make_async_remote_copy(
            src_ref=buffer.at[1, pl.ds(z_from, z_many), pl.ds(0, ROWS), :],
            dst_ref=buffer.at[1 - dx, pl.ds(z_to, z_many), pl.ds(y_to, ROWS), :],
            send_sem=send_sem.at[which, at_sem], recv_sem=recv_sem.at[which, at_sem],
            device_id=target(d), device_id_type=MESH)

    def opposite(d):
        return tuple(-c for c in d)

    for d in DIRECTIONS:
        @pl.when(exists(d))
        def _(d=d):
            velocity_copy(d).start()
            pressure_copy(scale_all, 1, d).start()

    start_v, steps_v = chebyshev_scalars(vbounds, SWEEPS)
    start_p, steps_p = chebyshev_scalars(pbounds, PITERS)

    for d in DIRECTIONS:
        @pl.when(exists(opposite(d)))
        def _(d=d):
            velocity_copy(d).wait_recv()
            pressure_copy(scale_all, 1, d).wait_recv()

    row8 = lax.broadcasted_iota(jnp.int32, (ROWS, nx), 0) < ROWS // 2
    wide_lane = lax.broadcasted_iota(jnp.int32, (ny + ROWS, nx), 1)
    from_right = lax.rem(wide_lane, GROUP) < GROUP // 2

    def fold_rows(block):
        low, up, down = block[:-2 * ROWS], block[-2 * ROWS:-ROWS], block[-ROWS:]
        return jnp.concatenate([low, jnp.where(row8[:, :block.shape[1]], up, down)], axis=0)

    @pl.loop(0, depth)
    def _(k):
        halo = jnp.where(from_right, fold_rows(right[k]), fold_rows(left[k]))

        def whole(f):
            side = pltpu.roll(halo, nx - GROUP * f, 1) if f else halo
            return jnp.concatenate([fold_rows(main[f, k]), side], axis=1)

        weight = whole(3)
        wide_v[k] = weight
        wide_m[k] = whole(4)
        for c in range(3):
            source = whole(c)
            wide_b[c, k] = source
            smooth[c, k] = average(average(weight * (source * start_v), 1, 0.5, 1.0), 0, 0.5, 1.0)

    def apply_wide(c, k, held, direction, weight):
        mean = held[c, k] + 0.5 * (held[c, k - 1] + held[c, k + 1])
        return weight * (16.0 * (weight * direction) - 2.0 * mean) + wide_m[k] * direction

    @pl.loop(1, depth - 1)
    def _(k):
        weight = wide_v[k]
        for c in range(3):
            source = wide_b[c, k]
            first = source * start_v
            rest = source - apply_wide(c, k, smooth, first, weight)
            second = steps_v[0][0] * first + steps_v[0][1] * rest
            resid[c, k] = rest
            direct[c, k] = second
            total[c, k] = first + second
            smooth_next[c, k] = average(average(weight * second, 1, 0.5, 1.0), 0, 0.5, 1.0)

    @pl.loop(2, depth - 2)
    def _(k):
        weight = wide_v[k]
        for c in range(3):
            second = direct[c, k]
            rest = resid[c, k] - apply_wide(c, k, smooth_next, second, weight)
            total[c, k] = total[c, k] + (steps_v[1][0] * second + steps_v[1][1] * rest)

    for c in range(3):
        vres[c] = total[c, mid, pl.ds(0, ny), pl.ds(0, nx)]
    store_velocity = pltpu.make_async_copy(vres, vout, local_sem.at[5])
    store_velocity.start()

    for k in range(pz):
        z = BELOW + 2 * k
        for c in range(2):
            gathered[c, k] = 0.5 * total[c, z] + 0.25 * (total[c, z - 1] + total[c, z + 1])
        gathered[2, k] = 0.25 * (total[2, z + 1] - total[2, z - 1]) + 0.125 * (
            total[2, z + 2] - total[2, z - 2])
    wide_rows = ny + ROWS

    def along_x(c, matrix):
        return jnp.dot(
            gathered[c].reshape(pz * wide_rows, 2 * nx), to_pressure[matrix],
            precision=lax.Precision.HIGHEST, preferred_element_type=jnp.float32,
        ).reshape(pz, wide_rows, 2 * px)

    part0, part1, part2 = along_x(0, 1), along_x(1, 0), along_x(2, 0)
    for k in range(pz):
        u = part1[k]
        one = pltpu.roll(u, wide_rows - 1, 0) - pltpu.roll(u, 1, 0)
        two = pltpu.roll(u, wide_rows - 2, 0) - pltpu.roll(u, 2, 0)
        rows_at[k] = average(part0[k] + part2[k], 0, 0.25, 0.5) + (0.25 * one + 0.125 * two)
    for k in range(pz):
        source = prhs_in[k]
        coupled_all[1, PITERS + k, pl.ds(0, py), :] = (
            jnp.concatenate([source, source], axis=1) - rows_at[k, pl.ds(0, py, stride=2), :])

    for d in DIRECTIONS:
        @pl.when(exists(d))
        def _(d=d):
            pressure_copy(coupled_all, 2, d).start()

    for d in DIRECTIONS:
        @pl.when(exists(opposite(d)))
        def _(d=d):
            pressure_copy(coupled_all, 2, d).wait_recv()

    narrow_lane = lax.broadcasted_iota(jnp.int32, (py + ROWS, 2 * px), 1)
    deep = pz + 2 * PITERS

    def whole_pressure(buffer, k):
        outside = jnp.where(
            narrow_lane < px + px // 2, fold_rows(buffer[2, k]), fold_rows(buffer[0, k]))
        return jnp.where(narrow_lane < px, fold_rows(buffer[1, k]), outside)

    scales = [whole_pressure(scale_all, k) for k in range(deep)]
    rest = [whole_pressure(coupled_all, k) for k in range(deep)]
    way = [value * start_p for value in rest]
    answer = list(way)
    for n in range(PITERS):
        mean = [
            average(average(scales[k] * way[k], 1, 1 / 6, 2 / 3), 0, 1 / 6, 2 / 3) if n <= k < deep - n else None
            for k in range(deep)]
        for k in range(n + 1, deep - n - 1):
            applied = scales[k] * ((2 / 3) * mean[k] + (1 / 6) * (mean[k - 1] + mean[k + 1]))
            rest[k] = rest[k] - applied
            way[k] = steps_p[n][0] * way[k] + steps_p[n][1] * rest[k]
            answer[k] = answer[k] + way[k]
    for k in range(pz):
        pres[k] = answer[PITERS + k][:py, :px]
    store_pressure = pltpu.make_async_copy(pres, pout, local_sem.at[6])
    store_pressure.start()

    for d in DIRECTIONS:
        @pl.when(exists(d))
        def _(d=d):
            velocity_copy(d).wait_send()
            pressure_copy(scale_all, 1, d).wait_send()
            pressure_copy(coupled_all, 2, d).wait_send()
    store_velocity.wait()
    store_pressure.wait()


def per_device(vrhs, prhs, visc, mass, pscale, vbounds, pbounds):
    nz, ny, nx = visc.shape
    pz, py, px = pscale.shape
    depth = BELOW + nz + ABOVE
    wide = (depth, ny + ROWS, 2 * nx)
    f32 = jnp.float32
    anywhere = pl.BlockSpec(memory_space=pl.ANY)
    scalars = pl.BlockSpec(memory_space=pltpu.SMEM)
    ways = len(DIRECTIONS)
    edge = (depth, ny + 2 * ROWS, nx)
    pressure_all = (3, pz + 2 * PITERS, py + 2 * ROWS, 2 * px)
    return pl.pallas_call(
        kernel,
        out_shape=(jax.ShapeDtypeStruct(vrhs.shape, f32), jax.ShapeDtypeStruct(prhs.shape, f32)),
        in_specs=[anywhere] * 5 + [scalars] * 2,
        out_specs=(anywhere, anywhere),
        scratch_shapes=[
            pltpu.VMEM((FIELDS,) + edge, f32),
            pltpu.VMEM(edge, f32),
            pltpu.VMEM(edge, f32),
            pltpu.VMEM((nz, ny, nx), f32),
            pltpu.VMEM((3,) + wide, f32),
            pltpu.VMEM(wide, f32),
            pltpu.VMEM(wide, f32),
            pltpu.VMEM((3,) + wide, f32),
            pltpu.VMEM((3,) + wide, f32),
            pltpu.VMEM((3,) + wide, f32),
            pltpu.VMEM((3,) + wide, f32),
            pltpu.VMEM((3,) + wide, f32),
            pltpu.VMEM((3, pz, ny + ROWS, 2 * nx), f32),
            pltpu.VMEM((pz, py, px), f32),
            pltpu.VMEM((pz, py, px), f32),
            pltpu.VMEM(pressure_all, f32),
            pltpu.VMEM(pressure_all, f32),
            pltpu.VMEM((2, 2 * nx, 2 * px), f32),
            pltpu.VMEM((pz, ny + ROWS, 2 * px), f32),
            pltpu.VMEM((3, nz, ny, nx), f32),
            pltpu.VMEM((pz, py, px), f32),
            pltpu.SemaphoreType.DMA((7,)),
            pltpu.SemaphoreType.DMA((3, ways)),
            pltpu.SemaphoreType.DMA((3, ways)),
        ],
        compiler_params=pltpu.CompilerParams(collective_id=0, has_side_effects=True),
    )(vrhs, prhs, visc, mass, pscale, vbounds, pbounds)


def solution(mesh):
    cells = P("gz", "gy", "gx")
    in_specs = (P(None, "gz", "gy", "gx"), cells, cells, cells, cells, P(), P())
    out_specs = (P(None, "gz", "gy", "gx"), cells)
    return jax.shard_map(
        per_device, mesh=mesh, in_specs=in_specs, out_specs=out_specs, check_vma=False
    )
```

time: 94.8 us -> 32.2 us (0.34)
  waiting for transfers between devices: 37 us -> 0 us
  starting transfers between devices: 36.7 us -> 0 us
  Pallas kernels: 0 us -> 29.2 us
  other arithmetic: 9.98 us -> 0 us
  between operations: 6.88 us -> 0.65 us
  local copies, waits for them, and re-layouts: 3.6 us -> 2.23 us
    ppermute x18 -> x0, waiting for transfers between devices: 37 us -> none  [the longest x9 33.6 us: with_halo(): after = lax.ppermute(leading, axis, down)]
    ppermute x18 -> x0, starting transfers between devices: 36.7 us -> none  [the longest x9 25.1 us: with_halo(): before = lax.ppermute(last, axis, up)]
    pallas_call x0 -> x1, Pallas kernels: none -> 29.2 us  [per_device(): pl.pallas_call(kernel, out_shape=(jax.ShapeDtypeStruct(vrhs.shape, f32),...]
    add x13 -> x0, other arithmetic: 6.25 us -> none  [the longest x8 3.33 us: smooth_three(): outer_weight * lax.slice_in_dim(result, 0, length, axis=dimension)]
    slice x15 -> x0, local copies, waits for them, and re-layouts: 3.5 us -> none  [the longest x2 1.23 us: chebyshev(): low_end = bounds[0]]
    unnamed x14 -> x4, local copies, waits for them, and re-layouts: 0.04 us -> 2.23 us
    concatenate x5 -> x0, other arithmetic: 2.16 us -> none  [the longest x4 1.1 us: with_halo(): value = jnp.concatenate([before, value, after], axis=dim)]
    mul x4 -> x0, other arithmetic: 1.08 us -> none  [the longest x2 0.99 us: apply_wide(): weighted = scale_wide * direction]
  transfers between devices with their start and end apart: 18 -> 0, of which waited for: 11 -> 0; matrix products, arithmetic and copies ran while one was open for 2% -> 0% of each run, Pallas kernels for 0% -> 0%
where the time goes in v1:
time: 32.2 us; the launch traced here: 32 us
  Pallas kernels  29.2 us (91%)
  local copies, waits for them, and re-layouts  2.23 us (7%)
  between operations  0.65 us (2%)
    pallas_call x1, Pallas kernels, per_device(): pl.pallas_call(kernel, out_shape=(jax.ShapeDtypeStruct(vrhs.shape, f32),...  29.2 us
    unnamed x4, local copies, waits for them, and re-layouts  2.23 us

profile of v1, /device:TPU:0, one launch (start us, length us, event | category | flops | bytes accessed | tf_op | source)
XLA Modules:
  0.0 32.0 jit_solution(12313415030725716708)
XLA Ops:
  0.6 29.2 %shard_map.86 = (f32[3,8,16,128]{3,2,1,0:T(8,128)}, f32[4,8,64]{2,1,0:T(8,128)}) custom-call(f32[3,8,16,128]{3,2,1,0:T(8,128)} %vrhs.1, f32[4,8,64]{2,1,0:T(8,128)} %prhs.1, f32[8,16,128]{2,1,0:T(8,128)} %visc.1, f32[8,16,128]{2,1,0:T(8,128)} %mass.1, f32[4,8,64]{2,1,0:T(8,128)} %pscale.1, f32[2]{0:T(128)} %vbounds.1, f32[2]{0:T(128)} %pbounds.1), custom_call_target="tpu_custom_call" | custom-call | tf_op jit(solution)/shard_map/pallas_call | solution.py:308
  29.8 0.0 copy-start
  29.8 1.6 %copy.11 = f32[3,8,16,128]{3,2,1,0:T(8,128)} copy(f32[3,8,16,128]{3,2,1,0:T(8,128)} %get-tuple-element.4) | data formatting | bytes 393216
  31.4 0.0 copy-done
  31.4 0.6 %copy.12 = f32[4,8,64]{2,1,0:T(8,128)} copy(f32[4,8,64]{2,1,0:T(8,128)S(1)} %copy-done) | data formatting | bytes 16384
Async XLA Ops:
  29.8 1.6 %copy-start = (f32[4,8,64]{2,1,0:T(8,128)S(1)}, f32[4,8,64]{2,1,0:T(8,128)}, u32[]{:S(2)}) copy-start(f32[4,8,64]{2,1,0:T(8,128)} %get-tuple-element.5) | copy-start | bytes 24580

commit v2 on v1

--- a/solution.py
+++ b/solution.py
@@ -13,6 +13,8 @@
 ABOVE = SWEEPS + 1
 ROWS = 8
 FIELDS = 5
+VISCOSITY, MASS, COMPONENT = 1, 4, (2, 3, 0)
+DEEP = 2
 GROUP = 8
 MESH = pl.DeviceIdType.MESH
 AXES = ("gx", "gy", "gz")
@@ -42,7 +44,7 @@
 def kernel(
     vrhs, prhs, visc, mass, pscale, vbounds, pbounds,
     vout, pout,
-    main, left, right, packed,
+    main, left, right, packed, ysend, yrecv,
     wide_b, wide_v, wide_m, smooth, smooth_next, resid, direct, total,
     gathered, prhs_in, pscale_in, scale_all, coupled_all, to_pressure, rows_at, vres, pres,
     local_sem, send_sem, recv_sem,
@@ -66,24 +68,16 @@
 
     mid = pl.ds(BELOW, nz)
     loads = [
-        pltpu.make_async_copy(vrhs, main.at[pl.ds(0, 3), mid, pl.ds(0, ny), :], local_sem.at[0]),
-        pltpu.make_async_copy(visc, main.at[3, mid, pl.ds(0, ny), :], local_sem.at[1]),
-        pltpu.make_async_copy(mass, main.at[4, mid, pl.ds(0, ny), :], local_sem.at[2]),
+        pltpu.make_async_copy(vrhs.at[pl.ds(0, 2)], main.at[pl.ds(2, 2), mid], local_sem.at[0]),
+        pltpu.make_async_copy(vrhs.at[2], main.at[0, mid], local_sem.at[7]),
+        pltpu.make_async_copy(visc, main.at[VISCOSITY, mid], local_sem.at[1]),
+        pltpu.make_async_copy(mass, main.at[MASS, mid], local_sem.at[2]),
         pltpu.make_async_copy(pscale, pscale_in, local_sem.at[3]),
         pltpu.make_async_copy(prhs, prhs_in, local_sem.at[4]),
     ]
     for load in loads:
         load.start()
 
-    for f in range(FIELDS):
-        main[f, pl.ds(0, BELOW)] = jnp.zeros((BELOW, ny + 2 * ROWS, nx), jnp.float32)
-        main[f, pl.ds(BELOW + nz, ABOVE)] = jnp.zeros((ABOVE, ny + 2 * ROWS, nx), jnp.float32)
-        main[f, mid, pl.ds(ny, 2 * ROWS)] = jnp.zeros((nz, 2 * ROWS, nx), jnp.float32)
-    left[...] = jnp.zeros_like(left)
-    right[...] = jnp.zeros_like(right)
-    scale_all[...] = jnp.zeros_like(scale_all)
-    coupled_all[...] = jnp.zeros_like(coupled_all)
-
     barrier = pltpu.get_barrier_semaphore()
     count = None
     for place, size in zip(at, sizes):
@@ -93,6 +87,42 @@
         @pl.when(exists(d))
         def _(d=d):
             pl.semaphore_signal(barrier, inc=1, device_id=target(d), device_id_type=MESH)
+
+    def clear(*refs):
+        for ref in refs:
+            ref[...] = jnp.zeros(ref.shape, jnp.float32)
+
+    for plane in (0, depth - 1):
+        for f in range(DEEP, FIELDS):
+            clear(main.at[f, plane])
+        for side in range(2):
+            for t in range(1, 3):
+                clear(yrecv.at[side, t, plane])
+
+    def missing(axis, sign):
+        return at[axis] == (0 if sign < 0 else sizes[axis] - 1)
+
+    for sign, buffer, slot in ((-1, left, 0), (1, right, 2)):
+        @pl.when(missing(0, sign))
+        def _(buffer=buffer, slot=slot):
+            clear(buffer, scale_all.at[slot], coupled_all.at[slot])
+
+    for sign, side in ((1, 0), (-1, 1)):
+        @pl.when(missing(1, sign))
+        def _(side=side):
+            rows = pl.ds(ny + side * ROWS, ROWS)
+            clear(yrecv.at[side], left.at[:, rows], right.at[:, rows])
+            rows = pl.ds(py + side * ROWS, ROWS)
+            clear(scale_all.at[:, :, rows], coupled_all.at[:, :, rows])
+
+    for sign, place, many, pplace in ((-1, 0, BELOW, 0), (1, BELOW + nz, ABOVE, PITERS + pz)):
+        @pl.when(missing(2, sign))
+        def _(place=place, many=many, pplace=pplace):
+            planes = pl.ds(place, many)
+            clear(main.at[:, planes], left.at[planes], right.at[planes])
+            clear(yrecv.at[0, :, planes], yrecv.at[1, :, planes])
+            planes = pl.ds(pplace, PITERS)
+            clear(scale_all.at[:, planes], coupled_all.at[:, planes])
 
     x_at = lax.broadcasted_iota(jnp.int32, (2 * nx, 2 * px), 0)
     x_at = jnp.where(x_at < nx + nx // 2, x_at, x_at - 2 * nx)
@@ -108,36 +138,59 @@
 
     lane = lax.broadcasted_iota(jnp.int32, (ny, nx), 1)
 
+    low_rows = lax.broadcasted_iota(jnp.int32, (ROWS, nx), 0) < ROWS // 2
+
     @pl.loop(0, nz)
     def _(k):
-        edge = main[0, BELOW + k, pl.ds(0, ny), :]
+        own = [main[f, BELOW + k] for f in range(FIELDS)]
+        edge = own[0]
         for f in range(1, FIELDS):
-            moved = pltpu.roll(main[f, BELOW + k, pl.ds(0, ny), :], GROUP * f, 1)
+            moved = pltpu.roll(own[f], GROUP * f, 1)
             inside = jnp.logical_and(lane >= GROUP * f - BELOW, lane < GROUP * f + BELOW)
             edge = jnp.where(inside, moved, edge)
         packed[k] = edge
+        for t in range(3):
+            low, high = own[2 * t][:ROWS], own[2 * t][-ROWS:]
+            if 2 * t + 1 < FIELDS:
+                other = own[2 * t + 1]
+                low = jnp.where(low_rows, low, pltpu.roll(other[:ROWS], ROWS // 2, 0))
+                high = jnp.where(low_rows, pltpu.roll(other[-ROWS:], ROWS // 2, 0), high)
+            ysend[0, t, k] = low
+            ysend[1, t, k] = high
 
     scale_own = pscale_in[...]
     scale_all[1, pl.ds(PITERS, pz), pl.ds(0, py), :] = jnp.concatenate([scale_own, scale_own], axis=2)
 
     pl.semaphore_wait(barrier, count - 1)
 
-    def velocity_copy(d):
+    def velocity_copies(d):
         dx, dy, dz = d
-        z_from, z_to, z_many = {
-            0: (BELOW, BELOW, nz), 1: (nz, 0, BELOW), -1: (BELOW, BELOW + nz, ABOVE)}[dz]
         y_from, y_to, y_many = {
             0: (0, 0, ny), 1: (ny - ROWS, ny + ROWS, ROWS), -1: (0, ny, ROWS)}[dy]
-        if dx == 0:
-            source = main.at[:, pl.ds(z_from, z_many), pl.ds(y_from, y_many), :]
-            place = main.at[:, pl.ds(z_to, z_many), pl.ds(y_to, y_many), :]
-        else:
-            source = packed.at[pl.ds(z_from - BELOW, z_many), pl.ds(y_from, y_many), :]
-            place = (left if dx == 1 else right).at[pl.ds(z_to, z_many), pl.ds(y_to, y_many), :]
-        at_sem = DIRECTIONS.index(d)
-        return pltpu.make_async_remote_copy(
-            src_ref=source, dst_ref=place, send_sem=send_sem.at[0, at_sem],
-            recv_sem=recv_sem.at[0, at_sem], device_id=target(d), device_id_type=MESH)
+        pieces = [(0, 0)] if dx or not dz else [(0, 0), (1, 1)]
+        copies = []
+        for group, cut in pieces:
+            z_from, z_to, z_many = {
+                0: (0, BELOW, nz), 1: (nz - BELOW + cut, cut, BELOW - cut),
+                -1: (0, BELOW + nz, ABOVE - cut)}[dz]
+            if dx:
+                source = packed.at[pl.ds(z_from, z_many), pl.ds(y_from, y_many), :]
+                place = (left if dx == 1 else right).at[pl.ds(z_to, z_many), pl.ds(y_to, y_many), :]
+            elif dy:
+                side = 1 if dy == 1 else 0
+                tiles = pl.ds(0, 3) if not dz else pl.ds(1, 2) if group else pl.ds(0, 1)
+                source = ysend.at[side, tiles, pl.ds(z_from, z_many)]
+                place = yrecv.at[side, tiles, pl.ds(z_to, z_many)]
+            else:
+                fields = pl.ds(DEEP, FIELDS - DEEP) if group else pl.ds(0, DEEP)
+                source = main.at[fields, pl.ds(BELOW + z_from, z_many)]
+                place = main.at[fields, pl.ds(z_to, z_many)]
+            at_sem = DIRECTIONS.index(d)
+            which = 3 if group else 0
+            copies.append(pltpu.make_async_remote_copy(
+                src_ref=source, dst_ref=place, send_sem=send_sem.at[which, at_sem],
+                recv_sem=recv_sem.at[which, at_sem], device_id=target(d), device_id_type=MESH))
+        return copies
 
     def pressure_copy(buffer, which, d):
         dx, dy, dz = d
@@ -157,17 +210,25 @@
     for d in DIRECTIONS:
         @pl.when(exists(d))
         def _(d=d):
-            velocity_copy(d).start()
+            for copy in velocity_copies(d):
+                copy.start()
+
+    for d in DIRECTIONS:
+        @pl.when(exists(d))
+        def _(d=d):
             pressure_copy(scale_all, 1, d).start()
 
     start_v, steps_v = chebyshev_scalars(vbounds, SWEEPS)
     start_p, steps_p = chebyshev_scalars(pbounds, PITERS)
 
-    for d in DIRECTIONS:
-        @pl.when(exists(opposite(d)))
-        def _(d=d):
-            velocity_copy(d).wait_recv()
-            pressure_copy(scale_all, 1, d).wait_recv()
+    def arrive(directions):
+        for d in directions:
+            @pl.when(exists(opposite(d)))
+            def _(d=d):
+                for copy in velocity_copies(d):
+                    copy.wait_recv()
+
+    arrive([d for d in DIRECTIONS if not d[2]])
 
     row8 = lax.broadcasted_iota(jnp.int32, (ROWS, nx), 0) < ROWS // 2
     wide_lane = lax.broadcasted_iota(jnp.int32, (ny + ROWS, nx), 1)
@@ -177,19 +238,23 @@
         low, up, down = block[:-2 * ROWS], block[-2 * ROWS:-ROWS], block[-ROWS:]
         return jnp.concatenate([low, jnp.where(row8[:, :block.shape[1]], up, down)], axis=0)
 
-    @pl.loop(0, depth)
-    def _(k):
+    def start_plane(k):
         halo = jnp.where(from_right, fold_rows(right[k]), fold_rows(left[k]))
 
         def whole(f):
             side = pltpu.roll(halo, nx - GROUP * f, 1) if f else halo
-            return jnp.concatenate([fold_rows(main[f, k]), side], axis=1)
-
-        weight = whole(3)
+            up, down = yrecv[0, f // 2, k], yrecv[1, f // 2, k]
+            if f % 2:
+                tile = pltpu.roll(jnp.where(row8, down, up), ROWS // 2, 0)
+            else:
+                tile = jnp.where(row8, up, down)
+            return jnp.concatenate([jnp.concatenate([main[f, k], tile], axis=0), side], axis=1)
+
+        weight = whole(VISCOSITY)
         wide_v[k] = weight
-        wide_m[k] = whole(4)
+        wide_m[k] = whole(MASS)
         for c in range(3):
-            source = whole(c)
+            source = whole(COMPONENT[c])
             wide_b[c, k] = source
             smooth[c, k] = average(average(weight * (source * start_v), 1, 0.5, 1.0), 0, 0.5, 1.0)
 
@@ -197,8 +262,7 @@
         mean = held[c, k] + 0.5 * (held[c, k - 1] + held[c, k + 1])
         return weight * (16.0 * (weight * direction) - 2.0 * mean) + wide_m[k] * direction
 
-    @pl.loop(1, depth - 1)
-    def _(k):
+    def first_sweep(k):
         weight = wide_v[k]
         for c in range(3):
             source = wide_b[c, k]
@@ -210,13 +274,23 @@
             total[c, k] = first + second
             smooth_next[c, k] = average(average(weight * second, 1, 0.5, 1.0), 0, 0.5, 1.0)
 
-    @pl.loop(2, depth - 2)
-    def _(k):
+    def second_sweep(k):
         weight = wide_v[k]
         for c in range(3):
             second = direct[c, k]
             rest = resid[c, k] - apply_wide(c, k, smooth_next, second, weight)
             total[c, k] = total[c, k] + (steps_v[1][0] * second + steps_v[1][1] * rest)
+
+    stages = (start_plane, first_sweep, second_sweep)
+    for n, stage in enumerate(stages):
+        pl.loop(BELOW + n, BELOW + nz - n)(stage)
+
+    arrive([d for d in DIRECTIONS if d[2]])
+
+    for n, stage in enumerate(stages):
+        @pl.loop(0, BELOW + ABOVE)
+        def _(i, n=n, stage=stage):
+            stage(i + jnp.where(i < BELOW, n, nz - n))
 
     for c in range(3):
         vres[c] = total[c, mid, pl.ds(0, ny), pl.ds(0, nx)]
@@ -254,8 +328,16 @@
             pressure_copy(coupled_all, 2, d).start()
 
     for d in DIRECTIONS:
+        @pl.when(exists(d))
+        def _(d=d):
+            for copy in velocity_copies(d):
+                copy.wait_send()
+            pressure_copy(scale_all, 1, d).wait_send()
+
+    for d in DIRECTIONS:
         @pl.when(exists(opposite(d)))
         def _(d=d):
+            pressure_copy(scale_all, 1, d).wait_recv()
             pressure_copy(coupled_all, 2, d).wait_recv()
 
     narrow_lane = lax.broadcasted_iota(jnp.int32, (py + ROWS, 2 * px), 1)
@@ -287,8 +369,6 @@
     for d in DIRECTIONS:
         @pl.when(exists(d))
         def _(d=d):
-            velocity_copy(d).wait_send()
-            pressure_copy(scale_all, 1, d).wait_send()
             pressure_copy(coupled_all, 2, d).wait_send()
     store_velocity.wait()
     store_pressure.wait()
@@ -311,10 +391,12 @@
         in_specs=[anywhere] * 5 + [scalars] * 2,
         out_specs=(anywhere, anywhere),
         scratch_shapes=[
-            pltpu.VMEM((FIELDS,) + edge, f32),
+            pltpu.VMEM((FIELDS, depth, ny, nx), f32),
             pltpu.VMEM(edge, f32),
             pltpu.VMEM(edge, f32),
             pltpu.VMEM((nz, ny, nx), f32),
+            pltpu.VMEM((2, 3, nz, ROWS, nx), f32),
+            pltpu.VMEM((2, 3, depth, ROWS, nx), f32),
             pltpu.VMEM((3,) + wide, f32),
             pltpu.VMEM(wide, f32),
             pltpu.VMEM(wide, f32),
@@ -332,9 +414,9 @@
             pltpu.VMEM((pz, ny + ROWS, 2 * px), f32),
             pltpu.VMEM((3, nz, ny, nx), f32),
             pltpu.VMEM((pz, py, px), f32),
-            pltpu.SemaphoreType.DMA((7,)),
-            pltpu.SemaphoreType.DMA((3, ways)),
-            pltpu.SemaphoreType.DMA((3, ways)),
+            pltpu.SemaphoreType.DMA((8,)),
+            pltpu.SemaphoreType.DMA((4, ways)),
+            pltpu.SemaphoreType.DMA((4, ways)),
         ],
         compiler_params=pltpu.CompilerParams(collective_id=0, has_side_effects=True),
     )(vrhs, prhs, visc, mass, pscale, vbounds, pbounds)

time: 32.2 us -> 29 us (0.901)
  Pallas kernels: 29.2 us -> 26 us
    pallas_call x1, Pallas kernels: 29.2 us -> 26 us  [per_device(): pl.pallas_call(kernel, out_shape=(jax.ShapeDtypeStruct(vrhs.shape, f32),...]
where the time goes in v2:
time: 29 us; the launch traced here: 28.8 us
  Pallas kernels  26 us (90%)
  local copies, waits for them, and re-layouts  2.23 us (8%)
  between operations  0.65 us (2%)
    pallas_call x1, Pallas kernels, per_device(): pl.pallas_call(kernel, out_shape=(jax.ShapeDtypeStruct(vrhs.shape, f32),...  26 us
    unnamed x4, local copies, waits for them, and re-layouts  2.23 us

profile of v2, /device:TPU:0, one launch (start us, length us, event | category | flops | bytes accessed | tf_op | source)
XLA Modules:
  0.0 28.8 jit_solution(16536843337332617806)
XLA Ops:
  0.6 26.0 %shard_map.86 = (f32[3,8,16,128]{3,2,1,0:T(8,128)}, f32[4,8,64]{2,1,0:T(8,128)}) custom-call(f32[3,8,16,128]{3,2,1,0:T(8,128)} %vrhs.1, f32[4,8,64]{2,1,0:T(8,128)} %prhs.1, f32[8,16,128]{2,1,0:T(8,128)} %visc.1, f32[8,16,128]{2,1,0:T(8,128)} %mass.1, f32[4,8,64]{2,1,0:T(8,128)} %pscale.1, f32[2]{0:T(128)} %vbounds.1, f32[2]{0:T(128)} %pbounds.1), custom_call_target="tpu_custom_call" | custom-call | tf_op jit(solution)/shard_map/pallas_call | solution.py:388
  26.6 0.0 copy-start
  26.6 1.6 %copy.11 = f32[3,8,16,128]{3,2,1,0:T(8,128)} copy(f32[3,8,16,128]{3,2,1,0:T(8,128)} %get-tuple-element.4) | data formatting | bytes 393216
  28.2 0.0 copy-done
  28.2 0.6 %copy.12 = f32[4,8,64]{2,1,0:T(8,128)} copy(f32[4,8,64]{2,1,0:T(8,128)S(1)} %copy-done) | data formatting | bytes 16384
Async XLA Ops:
  26.6 1.6 %copy-start = (f32[4,8,64]{2,1,0:T(8,128)S(1)}, f32[4,8,64]{2,1,0:T(8,128)}, u32[]{:S(2)}) copy-start(f32[4,8,64]{2,1,0:T(8,128)} %get-tuple-element.5) | copy-start | bytes 24580

commit v3 on v2

--- a/solution.py
+++ b/solution.py
@@ -15,11 +15,12 @@
 FIELDS = 5
 VISCOSITY, MASS, COMPONENT = 1, 4, (2, 3, 0)
 DEEP = 2
-GROUP = 8
+SPAN = 32
 MESH = pl.DeviceIdType.MESH
 AXES = ("gx", "gy", "gz")
 DIRECTIONS = [d for d in itertools.product((0, -1, 1), repeat=3) if d != (0, 0, 0)]
 DIRECTIONS.sort(key=lambda d: -sum(abs(c) for c in d))
+PLANE_FIRST = sorted(DIRECTIONS, key=lambda d: abs(d[2]))
 
 
 def chebyshev_scalars(bounds, count):
@@ -46,7 +47,7 @@
     vout, pout,
     main, left, right, packed, ysend, yrecv,
     wide_b, wide_v, wide_m, smooth, smooth_next, resid, direct, total,
-    gathered, prhs_in, pscale_in, scale_all, coupled_all, to_pressure, rows_at, vres, pres,
+    gathered, prhs_in, pscale_in, scale_all, coupled_all, edge_send, edge_recv, to_pressure, rows_at, vres, pres,
     local_sem, send_sem, recv_sem,
 ):
     nz, ny, nx = visc.shape
@@ -102,10 +103,10 @@
     def missing(axis, sign):
         return at[axis] == (0 if sign < 0 else sizes[axis] - 1)
 
-    for sign, buffer, slot in ((-1, left, 0), (1, right, 2)):
+    for sign, buffer, slot in ((-1, left, 0), (1, right, 1)):
         @pl.when(missing(0, sign))
         def _(buffer=buffer, slot=slot):
-            clear(buffer, scale_all.at[slot], coupled_all.at[slot])
+            clear(buffer, edge_recv.at[:, slot])
 
     for sign, side in ((1, 0), (-1, 1)):
         @pl.when(missing(1, sign))
@@ -113,16 +114,17 @@
             rows = pl.ds(ny + side * ROWS, ROWS)
             clear(yrecv.at[side], left.at[:, rows], right.at[:, rows])
             rows = pl.ds(py + side * ROWS, ROWS)
-            clear(scale_all.at[:, :, rows], coupled_all.at[:, :, rows])
+            clear(scale_all.at[:, rows], coupled_all.at[:, rows], edge_recv.at[:, :, :, rows])
 
     for sign, place, many, pplace in ((-1, 0, BELOW, 0), (1, BELOW + nz, ABOVE, PITERS + pz)):
         @pl.when(missing(2, sign))
-        def _(place=place, many=many, pplace=pplace):
+        def _(sign=sign, place=place, many=many, pplace=pplace):
             planes = pl.ds(place, many)
-            clear(main.at[:, planes], left.at[planes], right.at[planes])
+            clear(main.at[:, planes], left.at[place // BELOW], right.at[place // BELOW])
+            clear(edge_recv.at[:, :, 1 + sign])
             clear(yrecv.at[0, :, planes], yrecv.at[1, :, planes])
             planes = pl.ds(pplace, PITERS)
-            clear(scale_all.at[:, planes], coupled_all.at[:, planes])
+            clear(scale_all.at[planes], coupled_all.at[planes])
 
     x_at = lax.broadcasted_iota(jnp.int32, (2 * nx, 2 * px), 0)
     x_at = jnp.where(x_at < nx + nx // 2, x_at, x_at - 2 * nx)
@@ -136,19 +138,11 @@
     for load in loads:
         load.wait()
 
-    lane = lax.broadcasted_iota(jnp.int32, (ny, nx), 1)
-
     low_rows = lax.broadcasted_iota(jnp.int32, (ROWS, nx), 0) < ROWS // 2
 
     @pl.loop(0, nz)
     def _(k):
         own = [main[f, BELOW + k] for f in range(FIELDS)]
-        edge = own[0]
-        for f in range(1, FIELDS):
-            moved = pltpu.roll(own[f], GROUP * f, 1)
-            inside = jnp.logical_and(lane >= GROUP * f - BELOW, lane < GROUP * f + BELOW)
-            edge = jnp.where(inside, moved, edge)
-        packed[k] = edge
         for t in range(3):
             low, high = own[2 * t][:ROWS], own[2 * t][-ROWS:]
             if 2 * t + 1 < FIELDS:
@@ -158,8 +152,37 @@
             ysend[0, t, k] = low
             ysend[1, t, k] = high
 
-    scale_own = pscale_in[...]
-    scale_all[1, pl.ds(PITERS, pz), pl.ds(0, py), :] = jnp.concatenate([scale_own, scale_own], axis=2)
+    lane = lax.broadcasted_iota(jnp.int32, (ny, nx), 1)
+
+    @pl.loop(0, nz // BELOW)
+    def _(g):
+        edges = [jnp.zeros((ny, nx), jnp.float32)] * 2
+        for z in range(BELOW):
+            for f in range(FIELDS):
+                value = main[f, BELOW + BELOW * g + z]
+                at_lane = SPAN * z + BELOW * f
+                inside = jnp.logical_and(lane >= at_lane, lane < at_lane + BELOW)
+                for side in range(2):
+                    moved = pltpu.roll(value, at_lane + BELOW * side, 1) if at_lane + side else value
+                    edges[side] = jnp.where(inside, moved, edges[side])
+        for side in range(2):
+            packed[side, g] = edges[side]
+
+    def pack_pressure(which, planes):
+        edge = planes[0]
+        place = lax.broadcasted_iota(jnp.int32, (py, 2 * px), 1)
+        for z, value in enumerate(planes):
+            for side in range(2):
+                at_lane = 4 * z + 2 * side
+                inside = jnp.logical_and(place >= at_lane, place < at_lane + 2)
+                moved = pltpu.roll(value, 4 * (z + side), 1) if z + side else value
+                edge = jnp.where(inside, moved, edge)
+        edge_send[which] = edge
+
+    scale_own = [jnp.concatenate([pscale_in[k], pscale_in[k]], axis=1) for k in range(pz)]
+    for k in range(pz):
+        scale_all[PITERS + k, pl.ds(0, py), :] = scale_own[k]
+    pack_pressure(0, scale_own)
 
     pl.semaphore_wait(barrier, count - 1)
 
@@ -174,8 +197,12 @@
                 0: (0, BELOW, nz), 1: (nz - BELOW + cut, cut, BELOW - cut),
                 -1: (0, BELOW + nz, ABOVE - cut)}[dz]
             if dx:
-                source = packed.at[pl.ds(z_from, z_many), pl.ds(y_from, y_many), :]
-                place = (left if dx == 1 else right).at[pl.ds(z_to, z_many), pl.ds(y_to, y_many), :]
+                groups = nz // BELOW
+                g_from, g_to, g_many = {
+                    0: (0, 1, groups), 1: (groups - 1, 0, 1), -1: (0, groups + 1, 1)}[dz]
+                side = 1 if dx == 1 else 0
+                source = packed.at[side, pl.ds(g_from, g_many), pl.ds(y_from, y_many), :]
+                place = (left if side else right).at[pl.ds(g_to, g_many), pl.ds(y_to, y_many), :]
             elif dy:
                 side = 1 if dy == 1 else 0
                 tiles = pl.ds(0, 3) if not dz else pl.ds(1, 2) if group else pl.ds(0, 1)
@@ -198,16 +225,21 @@
             0: (PITERS, PITERS, pz), 1: (pz, 0, PITERS), -1: (PITERS, PITERS + pz, PITERS)}[dz]
         y_to = {0: 0, 1: 2 * ROWS, -1: ROWS}[dy]
         at_sem = DIRECTIONS.index(d)
+        if dx:
+            source = edge_send.at[which - 1]
+            place = edge_recv.at[which - 1, (1 - dx) // 2, 1 - dz, pl.ds(y_to, ROWS)]
+        else:
+            source = buffer.at[pl.ds(z_from, z_many), pl.ds(0, ROWS), :]
+            place = buffer.at[pl.ds(z_to, z_many), pl.ds(y_to, ROWS), :]
         return pltpu.make_async_remote_copy(
-            src_ref=buffer.at[1, pl.ds(z_from, z_many), pl.ds(0, ROWS), :],
-            dst_ref=buffer.at[1 - dx, pl.ds(z_to, z_many), pl.ds(y_to, ROWS), :],
+            src_ref=source, dst_ref=place,
             send_sem=send_sem.at[which, at_sem], recv_sem=recv_sem.at[which, at_sem],
             device_id=target(d), device_id_type=MESH)
 
     def opposite(d):
         return tuple(-c for c in d)
 
-    for d in DIRECTIONS:
+    for d in PLANE_FIRST:
         @pl.when(exists(d))
         def _(d=d):
             for copy in velocity_copies(d):
@@ -232,17 +264,21 @@
 
     row8 = lax.broadcasted_iota(jnp.int32, (ROWS, nx), 0) < ROWS // 2
     wide_lane = lax.broadcasted_iota(jnp.int32, (ny + ROWS, nx), 1)
-    from_right = lax.rem(wide_lane, GROUP) < GROUP // 2
+    from_right = wide_lane < nx // 2
 
     def fold_rows(block):
         low, up, down = block[:-2 * ROWS], block[-2 * ROWS:-ROWS], block[-ROWS:]
         return jnp.concatenate([low, jnp.where(row8[:, :block.shape[1]], up, down)], axis=0)
 
     def start_plane(k):
-        halo = jnp.where(from_right, fold_rows(right[k]), fold_rows(left[k]))
+        group = lax.div(k, BELOW)
+        shift = SPAN * (k - BELOW * group)
+        near = pltpu.roll(fold_rows(right[group]), lax.rem(nx - shift, nx), 1)
+        far = pltpu.roll(fold_rows(left[group]), nx - BELOW - shift, 1)
 
         def whole(f):
-            side = pltpu.roll(halo, nx - GROUP * f, 1) if f else halo
+            side = jnp.where(from_right, near, far) if not f else jnp.where(
+                from_right, pltpu.roll(near, nx - BELOW * f, 1), pltpu.roll(far, nx - BELOW * f, 1))
             up, down = yrecv[0, f // 2, k], yrecv[1, f // 2, k]
             if f % 2:
                 tile = pltpu.roll(jnp.where(row8, down, up), ROWS // 2, 0)
@@ -317,10 +353,13 @@
         one = pltpu.roll(u, wide_rows - 1, 0) - pltpu.roll(u, 1, 0)
         two = pltpu.roll(u, wide_rows - 2, 0) - pltpu.roll(u, 2, 0)
         rows_at[k] = average(part0[k] + part2[k], 0, 0.25, 0.5) + (0.25 * one + 0.125 * two)
+    coupled_own = []
     for k in range(pz):
         source = prhs_in[k]
-        coupled_all[1, PITERS + k, pl.ds(0, py), :] = (
+        coupled_own.append(
             jnp.concatenate([source, source], axis=1) - rows_at[k, pl.ds(0, py, stride=2), :])
+        coupled_all[PITERS + k, pl.ds(0, py), :] = coupled_own[k]
+    pack_pressure(1, coupled_own)
 
     for d in DIRECTIONS:
         @pl.when(exists(d))
@@ -343,13 +382,16 @@
     narrow_lane = lax.broadcasted_iota(jnp.int32, (py + ROWS, 2 * px), 1)
     deep = pz + 2 * PITERS
 
-    def whole_pressure(buffer, k):
-        outside = jnp.where(
-            narrow_lane < px + px // 2, fold_rows(buffer[2, k]), fold_rows(buffer[0, k]))
-        return jnp.where(narrow_lane < px, fold_rows(buffer[1, k]), outside)
-
-    scales = [whole_pressure(scale_all, k) for k in range(deep)]
-    rest = [whole_pressure(coupled_all, k) for k in range(deep)]
+    def whole_pressure(buffer, which, k):
+        slot, z = (0, pz - PITERS + k) if k < PITERS else (
+            (1, k - PITERS) if k < PITERS + pz else (2, k - PITERS - pz))
+        near = pltpu.roll(fold_rows(edge_recv[which, 1, slot]), px - 4 * z, 1)
+        far = pltpu.roll(fold_rows(edge_recv[which, 0, slot]), 2 * px - 4 - 4 * z, 1)
+        outside = jnp.where(narrow_lane < px + px // 2, near, far)
+        return jnp.where(narrow_lane < px, fold_rows(buffer[k]), outside)
+
+    scales = [whole_pressure(scale_all, 0, k) for k in range(deep)]
+    rest = [whole_pressure(coupled_all, 1, k) for k in range(deep)]
     way = [value * start_p for value in rest]
     answer = list(way)
     for n in range(PITERS):
@@ -383,8 +425,8 @@
     anywhere = pl.BlockSpec(memory_space=pl.ANY)
     scalars = pl.BlockSpec(memory_space=pltpu.SMEM)
     ways = len(DIRECTIONS)
-    edge = (depth, ny + 2 * ROWS, nx)
-    pressure_all = (3, pz + 2 * PITERS, py + 2 * ROWS, 2 * px)
+    edge = (nz // BELOW + 2, ny + 2 * ROWS, nx)
+    pressure_all = (pz + 2 * PITERS, py + 2 * ROWS, 2 * px)
     return pl.pallas_call(
         kernel,
         out_shape=(jax.ShapeDtypeStruct(vrhs.shape, f32), jax.ShapeDtypeStruct(prhs.shape, f32)),
@@ -394,7 +436,7 @@
             pltpu.VMEM((FIELDS, depth, ny, nx), f32),
             pltpu.VMEM(edge, f32),
             pltpu.VMEM(edge, f32),
-            pltpu.VMEM((nz, ny, nx), f32),
+            pltpu.VMEM((2, nz // BELOW, ny, nx), f32),
             pltpu.VMEM((2, 3, nz, ROWS, nx), f32),
             pltpu.VMEM((2, 3, depth, ROWS, nx), f32),
             pltpu.VMEM((3,) + wide, f32),
@@ -410,6 +452,8 @@
             pltpu.VMEM((pz, py, px), f32),
             pltpu.VMEM(pressure_all, f32),
             pltpu.VMEM(pressure_all, f32),
+            pltpu.VMEM((2, py, 2 * px), f32),
+            pltpu.VMEM((2, 2, 3, py + 2 * ROWS, 2 * px), f32),
             pltpu.VMEM((2, 2 * nx, 2 * px), f32),
             pltpu.VMEM((pz, ny + ROWS, 2 * px), f32),
             pltpu.VMEM((3, nz, ny, nx), f32),

time: 29 us -> 28.3 us (0.976)
  Pallas kernels: 26 us -> 25.1 us
    pallas_call x1, Pallas kernels: 26 us -> 25.1 us  [per_device(): pl.pallas_call(kernel, out_shape=(jax.ShapeDtypeStruct(vrhs.shape, f32),...]
where the time goes in v3:
time: 28.3 us; the launch traced here: 28 us
  Pallas kernels  25.1 us (89%)
  local copies, waits for them, and re-layouts  2.23 us (8%)
  between operations  0.65 us (2%)
    pallas_call x1, Pallas kernels, per_device(): pl.pallas_call(kernel, out_shape=(jax.ShapeDtypeStruct(vrhs.shape, f32),...  25.1 us
    unnamed x4, local copies, waits for them, and re-layouts  2.23 us

profile of v3, /device:TPU:0, one launch (start us, length us, event | category | flops | bytes accessed | tf_op | source)
XLA Modules:
  0.0 28.0 jit_solution(12116504432992231090)
XLA Ops:
  0.6 25.1 %shard_map.86 = (f32[3,8,16,128]{3,2,1,0:T(8,128)}, f32[4,8,64]{2,1,0:T(8,128)}) custom-call(f32[3,8,16,128]{3,2,1,0:T(8,128)} %vrhs.1, f32[4,8,64]{2,1,0:T(8,128)} %prhs.1, f32[8,16,128]{2,1,0:T(8,128)} %visc.1, f32[8,16,128]{2,1,0:T(8,128)} %mass.1, f32[4,8,64]{2,1,0:T(8,128)} %pscale.1, f32[2]{0:T(128)} %vbounds.1, f32[2]{0:T(128)} %pbounds.1), custom_call_target="tpu_custom_call" | custom-call | tf_op jit(solution)/shard_map/pallas_call | solution.py:430
  25.8 0.0 copy-start
  25.8 1.6 %copy.11 = f32[3,8,16,128]{3,2,1,0:T(8,128)} copy(f32[3,8,16,128]{3,2,1,0:T(8,128)} %get-tuple-element.4) | data formatting | bytes 393216
  27.4 0.0 copy-done
  27.4 0.6 %copy.12 = f32[4,8,64]{2,1,0:T(8,128)} copy(f32[4,8,64]{2,1,0:T(8,128)S(1)} %copy-done) | data formatting | bytes 16384
Async XLA Ops:
  25.8 1.6 %copy-start = (f32[4,8,64]{2,1,0:T(8,128)S(1)}, f32[4,8,64]{2,1,0:T(8,128)}, u32[]{:S(2)}) copy-start(f32[4,8,64]{2,1,0:T(8,128)} %get-tuple-element.5) | copy-start | bytes 24580

commit v4 on v3

--- a/solution.py
+++ b/solution.py
@@ -264,21 +264,22 @@
 
     row8 = lax.broadcasted_iota(jnp.int32, (ROWS, nx), 0) < ROWS // 2
     wide_lane = lax.broadcasted_iota(jnp.int32, (ny + ROWS, nx), 1)
-    from_right = wide_lane < nx // 2
 
     def fold_rows(block):
         low, up, down = block[:-2 * ROWS], block[-2 * ROWS:-ROWS], block[-ROWS:]
         return jnp.concatenate([low, jnp.where(row8[:, :block.shape[1]], up, down)], axis=0)
 
     def start_plane(k):
-        group = lax.div(k, BELOW)
+        group = k // BELOW
         shift = SPAN * (k - BELOW * group)
-        near = pltpu.roll(fold_rows(right[group]), lax.rem(nx - shift, nx), 1)
+        near = fold_rows(right[group])
+        near = pltpu.roll(near, nx - shift, 1) if shift else near
         far = pltpu.roll(fold_rows(left[group]), nx - BELOW - shift, 1)
 
         def whole(f):
-            side = jnp.where(from_right, near, far) if not f else jnp.where(
-                from_right, pltpu.roll(near, nx - BELOW * f, 1), pltpu.roll(far, nx - BELOW * f, 1))
+            from_right = jnp.logical_and(wide_lane >= BELOW * f, wide_lane < BELOW * f + nx // 2)
+            side = jnp.where(from_right, near, far)
+            side = pltpu.roll(side, nx - BELOW * f, 1) if f else side
             up, down = yrecv[0, f // 2, k], yrecv[1, f // 2, k]
             if f % 2:
                 tile = pltpu.roll(jnp.where(row8, down, up), ROWS // 2, 0)
@@ -319,14 +320,14 @@
 
     stages = (start_plane, first_sweep, second_sweep)
     for n, stage in enumerate(stages):
-        pl.loop(BELOW + n, BELOW + nz - n)(stage)
+        for k in range(BELOW + n, BELOW + nz - n):
+            stage(k)
 
     arrive([d for d in DIRECTIONS if d[2]])
 
     for n, stage in enumerate(stages):
-        @pl.loop(0, BELOW + ABOVE)
-        def _(i, n=n, stage=stage):
-            stage(i + jnp.where(i < BELOW, n, nz - n))
+        for i in range(BELOW + ABOVE):
+            stage(i + (n if i < BELOW else nz - n))
 
     for c in range(3):
         vres[c] = total[c, mid, pl.ds(0, ny), pl.ds(0, nx)]

time: 28.3 us -> 25.1 us (0.89)
  Pallas kernels: 25.1 us -> 21.9 us
    pallas_call x1, Pallas kernels: 25.1 us -> 21.9 us  [per_device(): pl.pallas_call(kernel, out_shape=(jax.ShapeDtypeStruct(vrhs.shape, f32),...]
where the time goes in v4:
time: 25.1 us; the launch traced here: 24.8 us
  Pallas kernels  21.9 us (87%)
  local copies, waits for them, and re-layouts  2.23 us (9%)
  between operations  0.65 us (3%)
    pallas_call x1, Pallas kernels, per_device(): pl.pallas_call(kernel, out_shape=(jax.ShapeDtypeStruct(vrhs.shape, f32),...  21.9 us
    unnamed x4, local copies, waits for them, and re-layouts  2.23 us

profile of v4, /device:TPU:0, one launch (start us, length us, event | category | flops | bytes accessed | tf_op | source)
XLA Modules:
  0.0 24.8 jit_solution(11403011446871592358)
XLA Ops:
  0.6 21.9 %shard_map.86 = (f32[3,8,16,128]{3,2,1,0:T(8,128)}, f32[4,8,64]{2,1,0:T(8,128)}) custom-call(f32[3,8,16,128]{3,2,1,0:T(8,128)} %vrhs.1, f32[4,8,64]{2,1,0:T(8,128)} %prhs.1, f32[8,16,128]{2,1,0:T(8,128)} %visc.1, f32[8,16,128]{2,1,0:T(8,128)} %mass.1, f32[4,8,64]{2,1,0:T(8,128)} %pscale.1, f32[2]{0:T(128)} %vbounds.1, f32[2]{0:T(128)} %pbounds.1), custom_call_target="tpu_custom_call" | custom-call | tf_op jit(solution)/shard_map/pallas_call | solution.py:431
  22.6 0.0 copy-start
  22.6 1.6 %copy.11 = f32[3,8,16,128]{3,2,1,0:T(8,128)} copy(f32[3,8,16,128]{3,2,1,0:T(8,128)} %get-tuple-element.4) | data formatting | bytes 393216
  24.2 0.0 copy-done
  24.2 0.6 %copy.12 = f32[4,8,64]{2,1,0:T(8,128)} copy(f32[4,8,64]{2,1,0:T(8,128)S(1)} %copy-done) | data formatting | bytes 16384
Async XLA Ops:
  22.6 1.6 %copy-start = (f32[4,8,64]{2,1,0:T(8,128)S(1)}, f32[4,8,64]{2,1,0:T(8,128)}, u32[]{:S(2)}) copy-start(f32[4,8,64]{2,1,0:T(8,128)} %get-tuple-element.5) | copy-start | bytes 24580
